TPU v7x, 128 devices: a whole 4x4x4 slice. The times are simulated.
128 devices in a mesh: gz: 128 (over y, z, x, core).
Axes of the slice: x: 4, y: 4, z: 4, core: 2. Of those that a mesh axis runs over, the one named last changes fastest.
Arguments:
- scores: int32 [512, 512, 512], P('gz'), may hold values from 0 to 134217727, as said below
Outputs:
- status: int32 [512, 512, 512], P('gz')
- counts: int32 [3], replicated
Inputs may be any that keep to these rules, and one draw needn't show every extreme that they name: `scores`: all values distinct: a permutation of 0 to 134217727.
All inputs are finite; a program needn't handle non-finite values.
Results may differ from a plain program's by a relative error of at most 0.000001.
Values may be sent and summed in bfloat16 or wider, within the bound.
No kernel may reach another device: no remote copies, remote signals or barrier semaphores. Data moves between devices by JAX's collectives and lax.ppermute only.
A program may use at most 64 MiB of HBM per device.

v0:
```python
import functools

import jax
import jax.numpy as jnp
from jax import lax
from jax.experimental import pallas as pl
from jax.experimental.pallas import tpu as pltpu
from jax.sharding import Mesh
from jax.sharding import PartitionSpec as P


GZ = ("gz_0", "gz_1", "gz_2", "gz_3")
LANES = 128
SUB = 8
VMEM = pltpu.VMEM
I32 = jnp.int32
U32 = jnp.int32
GRANT = pltpu.CompilerParams(vmem_limit_bytes=30 << 20)

EARLY = 3
BOX = 4


def in_vmem(x):
    return pltpu.with_memory_space_constraint(x, VMEM)


def smem():
    return pl.BlockSpec(memory_space=pltpu.SMEM)


def vmem(n):
    return [pl.BlockSpec(memory_space=VMEM)] * n


class Rows:
    def __init__(self, starts, refs):
        self.starts, self.refs = starts, refs

    def at(self, row):
        k = max(i for i, s in enumerate(self.starts) if s <= row)
        return self.refs[k], self.starts[k]


def for_rows(lo, hi, step, sources, body, unroll=1):
    edges = sorted({lo, hi, *[e for s in sources for e in s.starts if lo < e < hi]})
    for a, b in zip(edges, edges[1:]):
        def some(i, c, times, first, a=a):
            for u in range(times):
                r = first + (i * times + u) * step
                pick = lambda rows, r=r: (
                    rows.at(a)[0], pl.multiple_of(r - rows.at(a)[1], SUB)
                )
                body(r if isinstance(r, int) else pl.multiple_of(r, SUB), pick)
            return c

        groups = (b - a) // step
        whole = groups // unroll
        if whole:
            lax.fori_loop(0, whole, functools.partial(some, times=unroll, first=a), 0)
        if groups % unroll:
            some(0, 0, groups % unroll, a + whole * unroll * step)


def tile(c):
    return pl.ds(c * LANES, LANES)


def window(ref, index, first, count, op):
    out = ref[index, pl.ds(first - 2, count), :]
    for k in (-1, 0, 1, 2):
        out = op(out, ref[index, pl.ds(first + k, count), :])
    return out


def depth_maxima(p):
    mid = jnp.maximum(p[3], p[4])
    low = jnp.maximum(p[2], mid)
    all4 = jnp.maximum(low, p[5])
    return (
        jnp.maximum(low, jnp.maximum(p[0], p[1])),
        jnp.maximum(all4, p[1]),
        jnp.maximum(all4, p[6]),
        jnp.maximum(jnp.maximum(mid, p[5]), jnp.maximum(p[6], p[7])),
    )


def load_planes(pick, far, near, own, mate, c, inside):
    f, fr = pick(far)
    n, nr = pick(near)
    o, orow = pick(own)
    m, mr = pick(mate)
    get = lambda ref, k, r: ref[k, pl.ds(r, SUB), tile(c)].astype(U32)
    return [
        get(f, 1, fr) & inside,
        get(f, 0, fr) & inside,
        get(n, 0, nr),
        get(n, 1, nr),
        get(o, 1, orow),
        get(o, 0, orow),
        get(m, 0, mr),
        get(m, 1, mr),
    ]


def inside_mask(where):
    return jnp.full((SUB, LANES), where[1], I32).astype(U32)


def clear(ref, index, row):
    ref[index, pl.ds(row, SUB), :] = jnp.zeros((SUB, LANES), ref.dtype)


def cut_kernel(where, scores, *rest, parts, after):
    rest = rest[after:]
    outs, sems = rest[: len(parts)], rest[len(parts)]
    odd = where[0]
    copies = []
    for out, (kind, lo, hi) in zip(outs, parts):
        for k in range(2):
            j = k if kind == "near" else 3 - k
            plane = j + odd * (3 - 2 * j)
            copies.append(
                pltpu.make_async_copy(
                    scores.at[plane, pl.ds(lo, hi - lo), :], out.at[k], sems.at[len(copies)]
                )
            )
    for c in copies:
        c.start()
    for c in copies:
        c.wait()


def cut(where, scores, parts, after=()):
    width = scores.shape[2]
    return pl.pallas_call(
        functools.partial(cut_kernel, parts=parts, after=len(after)),
        compiler_params=GRANT,
        in_specs=[smem(), *[pl.BlockSpec(memory_space=pl.ANY)] * (1 + len(after))],
        out_specs=vmem(len(parts)),
        out_shape=[VMEM((2, hi - lo, width), I32) for _, lo, hi in parts],
        scratch_shapes=[pltpu.SemaphoreType.DMA((2 * len(parts),))],
    )(where, scores, *after)


def turn_kernel(*args, starts, height, tiles):
    near, own, out = Rows(starts, args[: len(starts)]), args[len(starts)], args[-1]
    for q in range(4):
        def body(b, carry, q=q):
            for c in range(tiles):
                rows = pl.ds(pl.multiple_of(b * LANES, LANES), LANES)
                block = own[3 - q, rows, tile(c)]
                out[q, b, pl.ds(c * LANES, LANES), :] = block.T
            return carry

        if q >= 2:
            lax.fori_loop(0, height // LANES, body, 0)
            continue
        for b in range(height // LANES):
            for c in range(tiles):
                pieces = []
                for s, e in zip(starts, (*starts[1:], height)):
                    lo, hi = max(s, b * LANES), min(e, (b + 1) * LANES)
                    if lo < hi:
                        pieces.append(near.at(lo)[0][q, pl.ds(lo - s, hi - lo), tile(c)])
                block = pieces[0] if len(pieces) == 1 else jnp.concatenate(pieces, axis=0)
                out[q, b, pl.ds(c * LANES, LANES), :] = block.T


def turn(starts, near, own):
    height, width = own.shape[1:]
    args = [in_vmem(x) for x in (*near, own)]
    return pl.pallas_call(
        functools.partial(turn_kernel, starts=starts, height=height, tiles=width // LANES),
        compiler_params=GRANT,
        in_specs=vmem(len(args)),
        out_specs=vmem(1)[0],
        out_shape=VMEM((4, height // LANES, width, LANES), I32),
    )(*args)


def box_columns(maxima, columns, first, tiles):
    def body(k, carry):
        wide = window(maxima, k, first, LANES, jnp.maximum)
        at = pl.multiple_of((k % tiles) * LANES, LANES) + SUB
        columns[k // tiles, pl.ds(at, LANES), :] = wide.T
        return carry

    lax.fori_loop(0, 4 * tiles, body, 0, unroll=BOX)


def roots_kernel(where, *args, spec):
    first, last, height, width, starts, n_far, n_before = spec
    tiles = width // LANES
    args = list(args)
    take = lambda n: [args.pop(0) for _ in range(n)]
    far, near = Rows(starts[:n_far], take(n_far)), Rows(starts, take(len(starts)))
    own, mate = Rows((0,), take(1)), Rows((0,), take(1))
    (turned,) = take(1)
    take(n_before)
    bits_out, far_out, mate_out, maxima, columns = args
    inside = inside_mask(where)
    lo, hi = first * LANES, last * LANES
    base = lo - SUB

    for k in range(4 * tiles):
        if lo == 0:
            clear(maxima, k, 0)
        if hi == height:
            clear(maxima, k, hi - base)
    for q in range(4):
        clear(columns, q, 0)
        clear(columns, q, SUB + width)

    def spread(r, pick):
        for c in range(tiles):
            deep = depth_maxima(load_planes(pick, far, near, own, mate, c, inside))
            for q in range(4):
                maxima[q * tiles + c, pl.ds(r - base, SUB), :] = deep[q]

    for_rows(max(lo - SUB, 0), min(hi + SUB, height), SUB, (far, near), spread, 2)

    for b in range(first, last):
        box_columns(maxima, columns, b * LANES - base, tiles)

        def decide(i, carry, b=b):
            at = pl.multiple_of(i * 2 * SUB, 2 * SUB)
            to_far, to_mate = [], []
            for half in range(2):
                bits = jnp.zeros((SUB, LANES), I32)
                ahead = behind = bits
                found = []
                for q in range(4):
                    box = window(columns, q, at + (half + 1) * SUB, SUB, jnp.maximum)
                    score = turned[q, b, pl.ds(at + half * SUB, SUB), :].astype(U32)
                    found.append(box == score)
                for q in range(4):
                    behind = jnp.where(found[q], q + 1, behind)
                    ahead = jnp.where(found[3 - q], q + 1, ahead)
                    bits = jnp.where(found[q], bits | ((31 << q) | (256 << q)), bits)
                bits_out[b, pl.ds(at + half * SUB, SUB), :] = bits
                to_far.append(ahead)
                to_mate.append(behind)
            both = pl.ds(at, 2 * SUB)
            far_out[b, both, :] = jnp.concatenate(to_far, axis=0).astype(jnp.int16)
            mate_out[b, both, :] = jnp.concatenate(to_mate, axis=0).astype(jnp.int16)
            return carry

        lax.fori_loop(0, width // (2 * SUB), decide, 0)


def find_roots(where, first, last, starts, far, near, own, mate, turned, before):
    height, width = own.shape[1:]
    args = [in_vmem(x) for x in (*far, *near, own, mate, turned, *before)]
    blocks = last - first
    shape = (height // LANES, width, LANES)
    spec = (first, last, height, width, starts, len(far), len(before))
    n = len(args) + 1 - len(before)
    return pl.pallas_call(
        functools.partial(roots_kernel, spec=spec),
        compiler_params=GRANT,
        in_specs=[smem(), *vmem(len(args))],
        out_specs=vmem(3),
        out_shape=[VMEM(shape, I32), VMEM(shape, jnp.int16), VMEM(shape, jnp.int16)],
        scratch_shapes=[
            VMEM((4 * width // LANES, blocks * LANES + 2 * SUB, LANES), U32),
            VMEM((4, width + 2 * SUB, LANES), U32),
        ],
        input_output_aliases={n + k: k for k in range(len(before))},
    )(where, *args)


def finish_kernel(where, *args, spec):
    height, width, starts = spec
    tiles, blocks = width // LANES, height // LANES
    args = list(args)
    take = lambda n: [args.pop(0) for _ in range(n)]
    far, near = Rows(starts, take(len(starts))), Rows(starts, take(len(starts)))
    own, mate = Rows((0,), take(1)), Rows((0,), take(1))
    (turned,) = take(1)
    bits, ahead, behind = take(3)
    status_out, count_out, reach, spots, gone, maxima, columns, marks, turned_marks, status, sems = args
    inside = inside_mask(where)
    odd = where[0]

    for k in range(4 * tiles):
        clear(maxima, k, 0)
        clear(maxima, k, SUB + height)
    for k in range(4):
        clear(columns, k, 0)
        clear(columns, k, SUB + width)
    for b in range(blocks):
        clear(reach, b, 0)
        clear(reach, b, SUB + width)
    for c in range(tiles):
        clear(spots, c, 0)
        clear(spots, c, SUB + height)

    def gather(i, carry):
        both = pl.ds(pl.multiple_of(i * 2 * SUB, 2 * SUB), 2 * SUB)
        for b in range(blocks):
            from_far = ahead[b, both, :].astype(I32)
            from_mate = behind[b, both, :].astype(I32)
            out = ((1 << from_far) - 1) | (256 - (256 >> from_mate)) | bits[b, both, :]
            reach[b, pl.ds(pl.multiple_of(i * 2 * SUB + SUB, SUB), 2 * SUB), :] = out
        return carry

    lax.fori_loop(0, width // (2 * SUB), gather, 0)

    def turn_back(b, carry):
        at = pl.multiple_of(SUB + b * LANES, SUB)
        for c in range(tiles):
            wide = window(reach, b, SUB + c * LANES, LANES, jnp.bitwise_or)
            spots[c, pl.ds(at, LANES), :] = wide.T
        return carry

    lax.fori_loop(0, blocks, turn_back, 0)

    def spread(r, pick):
        for c in range(tiles):
            removed = window(spots, c, r + SUB, SUB, jnp.bitwise_or)
            gone[c, pl.ds(r, SUB), :] = removed
            planes = load_planes(pick, far, near, own, mate, c, inside)
            left = [
                jnp.where((removed & (1 << k)) != 0, jnp.zeros_like(plane), plane)
                for k, plane in enumerate(planes)
            ]
            deep = depth_maxima(left)
            for q in range(4):
                maxima[q * tiles + c, pl.ds(r + SUB, SUB), :] = deep[q]

    for_rows(0, height, SUB, (far, near), spread, 2)

    copies = []
    zero = jnp.zeros((SUB, LANES), I32)
    carry = (zero, zero, zero)
    for b in range(blocks):
        box_columns(maxima, columns, SUB + b * LANES, tiles)

        def decide(i, c, b=b):
            at = pl.multiple_of(i * SUB, SUB)
            out = bits[b, pl.ds(at, SUB), :] & (15 << 8)
            for q in range(4):
                box = window(columns, q, at + SUB, SUB, jnp.maximum)
                score = turned[q, b, pl.ds(at, SUB), :].astype(U32)
                out = jnp.where(box == score, out | (1 << q), out)
            marks[pl.ds(at, SUB), :] = out
            return c

        lax.fori_loop(0, width // SUB, decide, 0, unroll=2)
        for c in range(tiles):
            turned_marks[c] = marks[pl.ds(c * LANES, LANES), :].T

        def settle(i, sums, b=b):
            at = pl.multiple_of(i * SUB, SUB)
            one, two, three = sums
            for c in range(tiles):
                mark = turned_marks[c, pl.ds(at, SUB), :]
                out = (gone[c, pl.ds(b * LANES + at, SUB), :] >> 2) & 15
                root = mark >> 8
                late = mark & 15 & ~out
                one = one + lax.population_count(root)
                two = two + lax.population_count(out)
                three = three + lax.population_count(out | late)
                ones, twos = root | late, out & ~root
                for q in range(4):
                    state = ((ones >> q) & 1) | (((twos << 1) >> q) & 2)
                    status[q, pl.ds(b * LANES + at, SUB), tile(c)] = state
            return one, two, three

        carry = lax.fori_loop(0, LANES // SUB, settle, carry)
        for q in range(4):
            copies.append(
                pltpu.make_async_copy(
                    status.at[q, pl.ds(b * LANES, LANES), :],
                    status_out.at[q + odd * (3 - 2 * q), pl.ds(b * LANES, LANES), :],
                    sems.at[4 * b + q],
                )
            )
            copies[-1].start()
    lane = lax.broadcasted_iota(I32, (1, LANES), 1)
    total = jnp.zeros((1, LANES), I32)
    for k in range(3):
        total = jnp.where(lane == k, 4 * height * width - jnp.sum(carry[k]), total)
    count_out[...] = jnp.broadcast_to(total, count_out.shape)
    for c in copies:
        c.wait()


def finish(where, starts, far, near, own, mate, turned, bits, ahead, behind, fan):
    height, width = own.shape[1:]
    tiles, blocks = width // LANES, height // LANES
    args = [in_vmem(x) for x in (*far, *near, own, mate, turned, bits, ahead, behind)]
    return pl.pallas_call(
        functools.partial(finish_kernel, spec=(height, width, starts)),
        compiler_params=GRANT,
        in_specs=[smem(), *vmem(len(args))],
        out_specs=[pl.BlockSpec(memory_space=pl.ANY), vmem(1)[0]],
        out_shape=[
            jax.ShapeDtypeStruct((4, height, width), I32),
            VMEM((fan, LANES), I32),
        ],
        scratch_shapes=[
            VMEM((blocks, width + 2 * SUB, LANES), I32),
            VMEM((tiles, height + 2 * SUB, LANES), I32),
            VMEM((tiles, height, LANES), I32),
            VMEM((4 * tiles, height + 2 * SUB, LANES), U32),
            VMEM((4, width + 2 * SUB, LANES), U32),
            VMEM((width, LANES), I32),
            VMEM((tiles, LANES, LANES), I32),
            VMEM((4, height, width), I32),
            pltpu.SemaphoreType.DMA((4 * blocks,)),
        ],
    )(where, *args)


def pairs(count, swap):
    return [(i, swap(i)) for i in range(count) if 0 <= swap(i) < count]


def shards(scores):
    count = lax.axis_size(GZ)
    height = scores.shape[1]
    blocks = height // LANES
    me = lax.axis_index(GZ)
    odd = me % 2
    edge = (me == 0) | (me == count - 1)
    where = jnp.stack([odd, jnp.where(edge, 0, -1)]).astype(I32)
    over = lambda x: lax.ppermute(x, GZ, pairs(count, lambda i: i - 1 + 2 * (i % 2)))
    swap = lambda x: lax.ppermute(x, GZ, pairs(count, lambda i: i ^ 1))

    early = EARLY if 0 < EARLY < blocks else 0
    starts = (0, early * LANES + SUB) if early else (0,)
    ends = (*starts[1:], height)
    firsts = (0, early) if early else (0,)
    lasts = (*firsts[1:], blocks)

    scores = pltpu.with_memory_space_constraint(scores, pltpu.HBM)
    near = [*cut(where, scores, (("near", 0, ends[0]),))]
    far = [over(near[0])]
    rest = [("near", a, b) for a, b in zip(starts[1:], ends[1:])]
    *more, own = cut(where, scores, (*rest, ("own", 0, height)), (in_vmem(near[0]),))
    near += more
    far += [over(x) for x in more]
    mate = swap(own)
    turned = turn(starts, near, own)

    found = ()
    for k, (a, b) in enumerate(zip(firsts, lasts)):
        found = find_roots(
            where, a, b, starts, far[: k + 1], near, own, mate, turned, found
        )
    bits, ahead, behind = found
    status, part = finish(
        where, starts, far, near, own, mate, turned, bits, over(ahead), swap(behind), count
    )
    total = jnp.sum(lax.all_to_all(part, GZ, 0, 0, tiled=True), axis=0)
    return status, total[:3]


def solution(mesh):
    finer = Mesh(mesh.devices.reshape(4, 4, 4, 2), GZ)
    return jax.shard_map(
        shards, mesh=finer, in_specs=(P(GZ, None, None),), out_specs=(P(GZ, None, None), P()),
        check_vma=False,
    )
```

profile of v0, /device:TPU:1, one launch (start us, length us, event | category | flops | bytes accessed | tf_op | source)
XLA Modules:
  0.0 86.4 jit_solution(5085471028891460557)
XLA Ops:
  0.7 0.1 pad_add_fusion.where
  0.7 1.9 %shard_map.30.rest_0_.args_0_.args_1_.args_2_ = s32[2,392,512]{2,1,0:T(8,128)S(1)} custom-call(s32[2]{0:T(128)S(1)} %pad_add_fusion.where, s32[4,512,512]{2,1,0:T(8,128)} %scores.3), custom_call_target="tpu_custom_call" | custom-call | tf_op jit(solution)/shard_map/pallas_call | solution.py:136
  2.7 2.4 %shard_map.31 = (s32[2,120,512]{2,1,0:T(8,128)S(1)}, s32[2,512,512]{2,1,0:T(8,128)S(1)}) custom-call(s32[2]{0:T(128)S(1)} %pad_add_fusion.where, s32[4,512,512]{2,1,0:T(8,128)} %scores.3, s32[2,392,512]{2,1,0:T(8,128)S(1)} %shard_map.30.rest_0_.args_0_.args_1_.args_2_), custom_call_target="tpu_custom_call" | custom-call | tf_op jit(solution)/shard_map/pallas_call | solution.py:136
  5.1 1.5 %collective-permute-start.2 = (s32[2,512,512]{2,1,0:T(8,128)S(1)}, s32[2,512,512]{2,1,0:T(8,128)S(1)}, u32[]{:S(2)}, u32[]{:S(2)}) collective-permute-start(s32[2,512,512]{2,1,0:T(8,128)S(1)} %get-tuple-element.13.args_2_.args_3_.args_4_), channel_id=1, source_target_pairs={{0,1},{1,0},{2,3},{3,2},{4,5},{5,4},{6,7},{7,6},{8,9},{9,8},{10,11... | collective-permute-start | bytes 6291464 | tf_op jit(solution)/shard_map/ppermute | solution.py:430
  6.5 3.1 %collective-permute-start = (s32[2,392,512]{2,1,0:T(8,128)S(1)}, s32[2,392,512]{2,1,0:T(8,128)S(1)}, u32[]{:S(2)}, u32[]{:S(2)}) collective-permute-start(s32[2,392,512]{2,1,0:T(8,128)S(1)} %shard_map.30.rest_0_.args_0_.args_1_.args_2_), channel_id=1, source_target_pairs={{1,2},{2,1},{3,4},{4,3},{5,6},{6,5},{7,8},{8,7},{9,10},{10,9},{11,... | collective-permute-start | bytes 4816904 | tf_op jit(solution)/shard_map/ppermute | solution.py:429
  9.7 2.4 %collective-permute-start.1 = (s32[2,120,512]{2,1,0:T(8,128)S(1)}, s32[2,120,512]{2,1,0:T(8,128)S(1)}, u32[]{:S(2)}, u32[]{:S(2)}) collective-permute-start(s32[2,120,512]{2,1,0:T(8,128)S(1)} %get-tuple-element.12.args_1_.args_2_.args_3_), channel_id=1, source_target_pairs={{1,2},{2,1},{3,4},{4,3},{5,6},{6,5},{7,8},{8,7},{9,10},{10,9},{11,... | collective-permute-start | bytes 1474568 | tf_op jit(solution)/shard_map/ppermute | solution.py:429
  12.1 1.7 %shard_map.32.args_5_.args_6_ = s32[4,4,512,128]{3,2,1,0:T(8,128)S(1)} custom-call(s32[2,392,512]{2,1,0:T(8,128)S(1)} %shard_map.30.rest_0_.args_0_.args_1_.args_2_, s32[2,120,512]{2,1,0:T(8,128)S(1)} %get-tuple-element.12.args_1_.args_2_.args_3_, s32[2,512,512]{2,1,0:T(8,128)S(1)} %get-tuple-element.13.args_2_.args_3_.args_4_), custom_call_target="tpu_custom_call" | custom-call | tf_op jit(solution)/shard_map/pallas_call | solution.py:173
  13.8 14.8 %collective-permute-done.args_0_ = s32[2,392,512]{2,1,0:T(8,128)S(1)} collective-permute-done((s32[2,392,512]{2,1,0:T(8,128)S(1)}, s32[2,392,512]{2,1,0:T(8,128)S(1)}, u32[]{:S(2)}, u32[]{:S(2)}) %collective-permute-start) | collective-permute-done | bytes 1605664 | tf_op jit(solution)/shard_map/ppermute | solution.py:429
  28.6 0.0 collective-permute-done.2.args_4_.args_5_
  28.6 5.2 %shard_map.33 = (s32[4,512,128]{2,1,0:T(8,128)S(1)}, s16[4,512,128]{2,1,0:T(8,128)(2,1)S(1)}, s16[4,512,128]{2,1,0:T(8,128)(2,1)S(1)}) custom-call(s32[2]{0:T(128)S(1)} %pad_add_fusion.where, s32[2,392,512]{2,1,0:T(8,128)S(1)} %collective-permute-done.args_0_, s32[2,392,512]{2,1,0:T(8,128)S(1)} %shard_map.30.rest_0_.args_0_.args_1_.args_2_, ...), custom_call_target="tpu_custom_call" | custom-call | tf_op jit(solution)/shard_map/pallas_call | solution.py:259
  33.8 0.1 collective-permute-done.1.args_1_
  33.9 2.1 %shard_map.34 = (s32[4,512,128]{2,1,0:T(8,128)S(1)}, s16[4,512,128]{2,1,0:T(8,128)(2,1)S(1)}, s16[4,512,128]{2,1,0:T(8,128)(2,1)S(1)}) custom-call(s32[2]{0:T(128)S(1)} %pad_add_fusion.where, s32[2,392,512]{2,1,0:T(8,128)S(1)} %collective-permute-done.args_0_, ...), custom_call_target="tpu_custom_call", output_to_operand_aliasing={{0}: (8, {}), {1}: (9, {}), {2}: (10, {})} | custom-call | tf_op jit(solution)/shard_map/pallas_call | solution.py:259
  36.0 3.1 %collective-permute-start.3 = (s16[4,512,128]{2,1,0:T(8,128)(2,1)S(1)}, s16[4,512,128]{2,1,0:T(8,128)(2,1)S(1)}, u32[]{:S(2)}, u32[]{:S(2)}) collective-permute-start(s16[4,512,128]{2,1,0:T(8,128)(2,1)S(1)} %get-tuple-element.18), channel_id=1, source_target_pairs={{1,2},{2,1},{3,4},{4,3},{5,6},{6,5},{7,8},{8,7},{9,10},{10,9},{11,... | collective-permute-start | bytes 1572872 | tf_op jit(solution)/shard_map/ppermute | solution.py:429
  39.1 0.1 collective-permute-start.4
  39.2 7.3 %collective-permute-done.3.args_8_ = s16[4,512,128]{2,1,0:T(8,128)(2,1)S(1)} collective-permute-done((s16[4,512,128]{2,1,0:T(8,128)(2,1)S(1)}, s16[4,512,128]{2,1,0:T(8,128)(2,1)S(1)}, u32[]{:S(2)}, u32[]{:S(2)}) %collective-permute-start.3) | collective-permute-done | bytes 524320 | tf_op jit(solution)/shard_map/ppermute | solution.py:429
  46.5 0.0 collective-permute-done.4.args_9_
  46.5 11.6 %shard_map.35 = (s32[4,512,512]{2,1,0:T(8,128)}, s32[128,128]{1,0:T(8,128)S(1)}) custom-call(s32[2]{0:T(128)S(1)} %pad_add_fusion.where, s32[2,392,512]{2,1,0:T(8,128)S(1)} %collective-permute-done.args_0_, s32[2,120,512]{2,1,0:T(8,128)S(1)} %collective-permute-done.1.args_1_, s32[2,392,512]{2,1,0:T(8,128)S(1)} %shard_map.30.rest_0_.args_0_.args_1_.args_2_, ...), custom_call_target="tpu_custom_call" | custom-call | tf_op jit(solution)/shard_map/pallas_call | solution.py:394
  58.1 27.7 %all_to_all.9 = s32[128,1,128]{2,1,0:T(1,128)S(1)} all-to-all(s32[128,1,128]{2,1,0:T(1,128)S(1)} %bitcast.6), channel_id=1, replica_groups=mesh['gz_0'=4,'gz_1'=4,'gz_2'=4,'gz_3'=2] {'gz_0','gz_1','gz_2','gz_3'}, dimensions={0} | all-to-all | bytes 131072 | tf_op jit(solution)/shard_map/all_to_all | solution.py:457
  85.8 0.7 reduce_sum.9
Async XLA Ops:
  5.1 23.5 %collective-permute-start.2 = (s32[2,512,512]{2,1,0:T(8,128)S(1)}, s32[2,512,512]{2,1,0:T(8,128)S(1)}, u32[]{:S(2)}, u32[]{:S(2)}) collective-permute-start(s32[2,512,512]{2,1,0:T(8,128)S(1)} %get-tuple-element.13.args_2_.args_3_.args_4_), channel_id=1, source_target_pairs={{0,1},{1,0},{2,3},{3,2},{4,5},{5,4},{6,7},{7,6},{8,9},{9,8},{10,11... | collective-permute-start | bytes 6291464 | tf_op jit(solution)/shard_map/ppermute | solution.py:430
  6.5 22.1 %collective-permute-start = (s32[2,392,512]{2,1,0:T(8,128)S(1)}, s32[2,392,512]{2,1,0:T(8,128)S(1)}, u32[]{:S(2)}, u32[]{:S(2)}) collective-permute-start(s32[2,392,512]{2,1,0:T(8,128)S(1)} %shard_map.30.rest_0_.args_0_.args_1_.args_2_), channel_id=1, source_target_pairs={{1,2},{2,1},{3,4},{4,3},{5,6},{6,5},{7,8},{8,7},{9,10},{10,9},{11,... | collective-permute-start | bytes 4816904 | tf_op jit(solution)/shard_map/ppermute | solution.py:429
  9.7 24.2 %collective-permute-start.1 = (s32[2,120,512]{2,1,0:T(8,128)S(1)}, s32[2,120,512]{2,1,0:T(8,128)S(1)}, u32[]{:S(2)}, u32[]{:S(2)}) collective-permute-start(s32[2,120,512]{2,1,0:T(8,128)S(1)} %get-tuple-element.12.args_1_.args_2_.args_3_), channel_id=1, source_target_pairs={{1,2},{2,1},{3,4},{4,3},{5,6},{6,5},{7,8},{8,7},{9,10},{10,9},{11,... | collective-permute-start | bytes 1474568 | tf_op jit(solution)/shard_map/ppermute | solution.py:429
  36.0 10.5 %collective-permute-start.3 = (s16[4,512,128]{2,1,0:T(8,128)(2,1)S(1)}, s16[4,512,128]{2,1,0:T(8,128)(2,1)S(1)}, u32[]{:S(2)}, u32[]{:S(2)}) collective-permute-start(s16[4,512,128]{2,1,0:T(8,128)(2,1)S(1)} %get-tuple-element.18), channel_id=1, source_target_pairs={{1,2},{2,1},{3,4},{4,3},{5,6},{6,5},{7,8},{8,7},{9,10},{10,9},{11,... | collective-permute-start | bytes 1572872 | tf_op jit(solution)/shard_map/ppermute | solution.py:429
  39.1 7.4 %collective-permute-start.4 = (s16[4,512,128]{2,1,0:T(8,128)(2,1)S(1)}, s16[4,512,128]{2,1,0:T(8,128)(2,1)S(1)}, u32[]{:S(2)}, u32[]{:S(2)}) collective-permute-start(s16[4,512,128]{2,1,0:T(8,128)(2,1)S(1)} %get-tuple-element.19), channel_id=1, source_target_pairs={{0,1},{1,0},{2,3},{3,2},{4,5},{5,4},{6,7},{7,6},{8,9},{9,8},{10,11... | collective-permute-start | bytes 1572872 | tf_op jit(solution)/shard_map/ppermute | solution.py:430
where the time goes:
time: 86.7 us; the launch traced here: 86.4 us
  blocking collectives  27.7 us (32%)
  Pallas kernels  24.8 us (29%)
  waiting for transfers between devices  22.2 us (26%)
  starting transfers between devices  10.2 us (12%)
    all_to_all x1, blocking collectives, shards(): total = jnp.sum(lax.all_to_all(part, GZ, 0, 0, tiled=True), axis=0)  27.7 us
    ppermute x3, waiting for transfers between devices, shards(): lax.ppermute(x, GZ, pairs(count, lambda i: i - 1 + 2 * (i % 2)))  22.2 us
    pallas_call x1, Pallas kernels, finish(): pl.pallas_call(functools.partial(finish_kernel, spec=(height, width, star...  11.6 us
    ppermute x3, starting transfers between devices, shards(): lax.ppermute(x, GZ, pairs(count, lambda i: i - 1 + 2 * (i % 2)))  8.69 us
    pallas_call x2, Pallas kernels, find_roots(): pl.pallas_call(functools.partial(roots_kernel, spec=spec), compiler_param...  7.24 us
    pallas_call x2, Pallas kernels, cut(): pl.pallas_call(functools.partial(cut_kernel, parts=parts, after=len(after...  4.32 us
  transfers between devices with their start and end apart: 5, of which 3 were waited for; matrix products, arithmetic and copies ran while one was open for 0% of the time, Pallas kernels for 8%

commit v1 on v0

--- a/solution.py
+++ b/solution.py
@@ -18,7 +18,9 @@
 GRANT = pltpu.CompilerParams(vmem_limit_bytes=30 << 20)
 
 EARLY = 3
-BOX = 4
+SCORE_BITS = 27
+SPARE = 32 - SCORE_BITS
+BOX = 16
 
 
 def in_vmem(x):
@@ -111,9 +113,79 @@
     ref[index, pl.ds(row, SUB), :] = jnp.zeros((SUB, LANES), ref.dtype)
 
 
-def cut_kernel(where, scores, *rest, parts, after):
+def packed_rows(rows):
+    groups = rows // SUB
+    return SUB * (groups - groups // 7)
+
+
+def for_groups(rows, body):
+    whole = rows // SUB // 7
+
+    def one(i, carry):
+        body(pl.multiple_of(i * 7 * SUB, SUB), pl.multiple_of(i * 6 * SUB, SUB), True)
+        return carry
+
+    if whole:
+        lax.fori_loop(0, whole, one, 0)
+    for j in range(rows // SUB - 7 * whole):
+        body((7 * whole + j) * SUB, (6 * whole + j) * SUB, False)
+
+
+def pack(src, dst, rows, tiles):
+    def body(r, w, whole):
+        for k in range(2):
+            for c in range(tiles):
+                get = lambda j: src[k, pl.ds(r + j * SUB, SUB), tile(c)]
+                if not whole:
+                    dst[k, pl.ds(w, SUB), tile(c)] = get(0)
+                    continue
+                last = get(6)
+                for j in range(6):
+                    part = lax.shift_left(
+                        lax.shift_right_logical(last, SPARE * j), SCORE_BITS
+                    )
+                    dst[k, pl.ds(w + j * SUB, SUB), tile(c)] = get(j) | part
+
+    for_groups(rows, body)
+
+
+def unpack_kernel(src, *rest, rows, tiles):
+    dst = rest[-1]
+
+    def body(r, w, whole):
+        for k in range(2):
+            for c in range(tiles):
+                get = lambda j: src[k, pl.ds(w + j * SUB, SUB), tile(c)]
+                if not whole:
+                    dst[k, pl.ds(r, SUB), tile(c)] = get(0)
+                    continue
+                last = jnp.zeros((SUB, LANES), I32)
+                for j in range(6):
+                    word = get(j)
+                    dst[k, pl.ds(r + j * SUB, SUB), tile(c)] = word & ((1 << SCORE_BITS) - 1)
+                    part = lax.shift_right_logical(word, SCORE_BITS)
+                    last = last | lax.shift_left(part, SPARE * j)
+                dst[k, pl.ds(r + 6 * SUB, SUB), tile(c)] = last
+
+    for_groups(rows, body)
+
+
+def unpack(words, rows, after=()):
+    width = words.shape[2]
+    return pl.pallas_call(
+        functools.partial(unpack_kernel, rows=rows, tiles=width // LANES),
+        compiler_params=GRANT,
+        in_specs=[*vmem(1), *[pl.BlockSpec(memory_space=pl.ANY)] * len(after)],
+        out_specs=vmem(1)[0],
+        out_shape=VMEM((2, rows, width), I32),
+    )(in_vmem(words), *[in_vmem(x) for x in after])
+
+
+def cut_kernel(where, scores, *rest, parts, after, tiles):
     rest = rest[after:]
-    outs, sems = rest[: len(parts)], rest[len(parts)]
+    n_packed = sum(kind == "near" for kind, _, _ in parts)
+    outs, packed = rest[: len(parts)], list(rest[len(parts) : len(parts) + n_packed])
+    sems = rest[len(parts) + n_packed]
     odd = where[0]
     copies = []
     for out, (kind, lo, hi) in zip(outs, parts):
@@ -127,20 +199,28 @@
             )
     for c in copies:
         c.start()
-    for c in copies:
-        c.wait()
+    for i, (out, (kind, lo, hi)) in enumerate(zip(outs, parts)):
+        copies[2 * i].wait()
+        copies[2 * i + 1].wait()
+        if kind == "near":
+            pack(out, packed.pop(0), hi - lo, tiles)
 
 
 def cut(where, scores, parts, after=()):
     width = scores.shape[2]
-    return pl.pallas_call(
-        functools.partial(cut_kernel, parts=parts, after=len(after)),
+    sent = [hi - lo for kind, lo, hi in parts if kind == "near"]
+    out = pl.pallas_call(
+        functools.partial(cut_kernel, parts=parts, after=len(after), tiles=width // LANES),
         compiler_params=GRANT,
         in_specs=[smem(), *[pl.BlockSpec(memory_space=pl.ANY)] * (1 + len(after))],
-        out_specs=vmem(len(parts)),
-        out_shape=[VMEM((2, hi - lo, width), I32) for _, lo, hi in parts],
+        out_specs=vmem(len(parts) + len(sent)),
+        out_shape=[
+            *[VMEM((2, hi - lo, width), I32) for _, lo, hi in parts],
+            *[VMEM((2, packed_rows(n), width), I32) for n in sent],
+        ],
         scratch_shapes=[pltpu.SemaphoreType.DMA((2 * len(parts),))],
     )(where, scores, *after)
+    return out[: len(parts)], out[len(parts) :]
 
 
 def turn_kernel(*args, starts, height, tiles):
@@ -246,7 +326,7 @@
             mate_out[b, both, :] = jnp.concatenate(to_mate, axis=0).astype(jnp.int16)
             return carry
 
-        lax.fori_loop(0, width // (2 * SUB), decide, 0)
+        lax.fori_loop(0, width // (2 * SUB), decide, 0, unroll=2)
 
 
 def find_roots(where, first, last, starts, far, near, own, mate, turned, before):
@@ -305,7 +385,7 @@
             reach[b, pl.ds(pl.multiple_of(i * 2 * SUB + SUB, SUB), 2 * SUB), :] = out
         return carry
 
-    lax.fori_loop(0, width // (2 * SUB), gather, 0)
+    lax.fori_loop(0, width // (2 * SUB), gather, 0, unroll=2)
 
     def turn_back(b, carry):
         at = pl.multiple_of(SUB + b * LANES, SUB)
@@ -314,7 +394,7 @@
             spots[c, pl.ds(at, LANES), :] = wide.T
         return carry
 
-    lax.fori_loop(0, blocks, turn_back, 0)
+    lax.fori_loop(0, blocks, turn_back, 0, unroll=2)
 
     def spread(r, pick):
         for c in range(tiles):
@@ -347,7 +427,7 @@
             marks[pl.ds(at, SUB), :] = out
             return c
 
-        lax.fori_loop(0, width // SUB, decide, 0, unroll=2)
+        lax.fori_loop(0, width // SUB, decide, 0, unroll=4)
         for c in range(tiles):
             turned_marks[c] = marks[pl.ds(c * LANES, LANES), :].T
 
@@ -368,7 +448,7 @@
                     status[q, pl.ds(b * LANES + at, SUB), tile(c)] = state
             return one, two, three
 
-        carry = lax.fori_loop(0, LANES // SUB, settle, carry)
+        carry = lax.fori_loop(0, LANES // SUB, settle, carry, unroll=2)
         for q in range(4):
             copies.append(
                 pltpu.make_async_copy(
@@ -430,26 +510,27 @@
     swap = lambda x: lax.ppermute(x, GZ, pairs(count, lambda i: i ^ 1))
 
     early = EARLY if 0 < EARLY < blocks else 0
-    starts = (0, early * LANES + SUB) if early else (0,)
+    starts = (0, early * LANES + SUB)
     ends = (*starts[1:], height)
-    firsts = (0, early) if early else (0,)
-    lasts = (*firsts[1:], blocks)
+    firsts, lasts = (0, early), (early, blocks)
 
     scores = pltpu.with_memory_space_constraint(scores, pltpu.HBM)
-    near = [*cut(where, scores, (("near", 0, ends[0]),))]
-    far = [over(near[0])]
+    near, words = cut(where, scores, (("near", 0, ends[0]),))
+    far = [unpack(over(words[0]), ends[0])]
     rest = [("near", a, b) for a, b in zip(starts[1:], ends[1:])]
-    *more, own = cut(where, scores, (*rest, ("own", 0, height)), (in_vmem(near[0]),))
-    near += more
-    far += [over(x) for x in more]
+    (*more, own), words = cut(
+        where, scores, (*rest, ("own", 0, height)), (in_vmem(near[0]),)
+    )
+    near = [*near, *more]
+    late = over(words[0])
     mate = swap(own)
     turned = turn(starts, near, own)
 
     found = ()
-    for k, (a, b) in enumerate(zip(firsts, lasts)):
-        found = find_roots(
-            where, a, b, starts, far[: k + 1], near, own, mate, turned, found
-        )
+    for a, b in zip(firsts, lasts):
+        if a:
+            far.append(unpack(late, height - starts[1], (found[0],)))
+        found = find_roots(where, a, b, starts, far, near, own, mate, turned, found)
     bits, ahead, behind = found
     status, part = finish(
         where, starts, far, near, own, mate, turned, bits, over(ahead), swap(behind), count

time: 86.7 us -> 82.1 us (0.947)
  waiting for transfers between devices: 22.2 us -> 19.7 us
  Pallas kernels: 24.8 us -> 22.7 us
    ppermute x3, waiting for transfers between devices: 22.2 us -> 19.7 us  [shards(): lax.ppermute(x, GZ, pairs(count, lambda i: i - 1 + 2 * (i % 2)))]
    pallas_call x1, Pallas kernels: 11.6 us -> 10.1 us  [finish(): pl.pallas_call(functools.partial(finish_kernel, spec=(height, width, star...]
    pallas_call x2, Pallas kernels: 7.24 us -> 5.98 us  [find_roots(): pl.pallas_call(functools.partial(roots_kernel, spec=spec), compiler_param...]
  transfers between devices with their start and end apart: 5 -> 5, of which waited for: 3 -> 3; matrix products, arithmetic and copies ran while one was open for 0% -> 0% of each run, Pallas kernels for 8% -> 7%
where the time goes in v1:
time: 82.1 us; the launch traced here: 81.9 us
  blocking collectives  27.7 us (34%)
  Pallas kernels  22.7 us (28%)
  waiting for transfers between devices  19.7 us (24%)
  starting transfers between devices  10.2 us (12%)
    all_to_all x1, blocking collectives, shards(): total = jnp.sum(lax.all_to_all(part, GZ, 0, 0, tiled=True), axis=0)  27.7 us
    ppermute x3, waiting for transfers between devices, shards(): lax.ppermute(x, GZ, pairs(count, lambda i: i - 1 + 2 * (i % 2)))  19.7 us
    pallas_call x1, Pallas kernels, finish(): pl.pallas_call(functools.partial(finish_kernel, spec=(height, width, star...  10.1 us
    ppermute x3, starting transfers between devices, shards(): lax.ppermute(x, GZ, pairs(count, lambda i: i - 1 + 2 * (i % 2)))  8.69 us
    pallas_call x2, Pallas kernels, find_roots(): pl.pallas_call(functools.partial(roots_kernel, spec=spec), compiler_param...  5.98 us
    pallas_call x2, Pallas kernels, cut(): pl.pallas_call(functools.partial(cut_kernel, parts=parts, after=len(after...  4.58 us
    pallas_call x1, Pallas kernels, turn(): pl.pallas_call(functools.partial(turn_kernel, starts=starts, height=heigh...  1.67 us
  transfers between devices with their start and end apart: 5, of which 3 were waited for; matrix products, arithmetic and copies ran while one was open for 0% of the time, Pallas kernels for 7%

profile of v1, /device:TPU:1, one launch (start us, length us, event | category | flops | bytes accessed | tf_op | source)
XLA Modules:
  0.0 81.9 jit_solution(8577070444938321899)
XLA Ops:
  0.7 0.1 pad_add_fusion.where
  0.7 2.2 %shard_map.30 = (s32[2,392,512]{2,1,0:T(8,128)S(1)}, s32[2,336,512]{2,1,0:T(8,128)S(1)}) custom-call(s32[2]{0:T(128)S(1)} %pad_add_fusion.where, s32[4,512,512]{2,1,0:T(8,128)} %scores.3), custom_call_target="tpu_custom_call" | custom-call | tf_op jit(solution)/shard_map/pallas_call | solution.py:212
  2.9 2.4 %shard_map.32 = (s32[2,120,512]{2,1,0:T(8,128)S(1)}, s32[2,512,512]{2,1,0:T(8,128)S(1)}, s32[2,104,512]{2,1,0:T(8,128)S(1)}) custom-call(s32[2]{0:T(128)S(1)} %pad_add_fusion.where, s32[4,512,512]{2,1,0:T(8,128)} %scores.3, s32[2,392,512]{2,1,0:T(8,128)S(1)} %get-tuple-element.16.rest_0_.args_0_.args_1_.args_2_), custom_call_target="tpu_custom_call" | custom-call | tf_op jit(solution)/shard_map/pallas_call | solution.py:212
  5.3 1.5 %collective-permute-start.2 = (s32[2,512,512]{2,1,0:T(8,128)S(1)}, s32[2,512,512]{2,1,0:T(8,128)S(1)}, u32[]{:S(2)}, u32[]{:S(2)}) collective-permute-start(s32[2,512,512]{2,1,0:T(8,128)S(1)} %get-tuple-element.19.args_2_.args_3_.args_4_), channel_id=1, source_target_pairs={{0,1},{1,0},{2,3},{3,2},{4,5},{5,4},{6,7},{7,6},{8,9},{9,8},{10,11... | collective-permute-start | bytes 6291464 | tf_op jit(solution)/shard_map/ppermute | solution.py:510
  6.8 3.1 %collective-permute-start = (s32[2,336,512]{2,1,0:T(8,128)S(1)}, s32[2,336,512]{2,1,0:T(8,128)S(1)}, u32[]{:S(2)}, u32[]{:S(2)}) collective-permute-start(s32[2,336,512]{2,1,0:T(8,128)S(1)} %get-tuple-element.15), channel_id=1, source_target_pairs={{1,2},{2,1},{3,4},{4,3},{5,6},{6,5},{7,8},{8,7},{9,10},{10,9},{11,... | collective-permute-start | bytes 4128776 | tf_op jit(solution)/shard_map/ppermute | solution.py:509
  9.9 2.4 %collective-permute-start.1 = (s32[2,104,512]{2,1,0:T(8,128)S(1)}, s32[2,104,512]{2,1,0:T(8,128)S(1)}, u32[]{:S(2)}, u32[]{:S(2)}) collective-permute-start(s32[2,104,512]{2,1,0:T(8,128)S(1)} %get-tuple-element.17), channel_id=1, source_target_pairs={{1,2},{2,1},{3,4},{4,3},{5,6},{6,5},{7,8},{8,7},{9,10},{10,9},{11,... | collective-permute-start | bytes 1277960 | tf_op jit(solution)/shard_map/ppermute | solution.py:509
  12.4 1.7 %shard_map.33.args_5_.args_6_ = s32[4,4,512,128]{3,2,1,0:T(8,128)S(1)} custom-call(s32[2,392,512]{2,1,0:T(8,128)S(1)} %get-tuple-element.16.rest_0_.args_0_.args_1_.args_2_, s32[2,120,512]{2,1,0:T(8,128)S(1)} %get-tuple-element.18.args_1_.args_2_.args_3_, s32[2,512,512]{2,1,0:T(8,128)S(1)} %get-tuple-element.19.args_2_.args_3_.args_4_), custom_call_target="tpu_custom_call" | custom-call | tf_op jit(solution)/shard_map/pallas_call | solution.py:253
  14.0 12.4 %collective-permute-done.src = s32[2,336,512]{2,1,0:T(8,128)S(1)} collective-permute-done((s32[2,336,512]{2,1,0:T(8,128)S(1)}, s32[2,336,512]{2,1,0:T(8,128)S(1)}, u32[]{:S(2)}, u32[]{:S(2)}) %collective-permute-start) | collective-permute-done | bytes 1376288 | tf_op jit(solution)/shard_map/ppermute | solution.py:509
  26.4 0.3 shard_map.31.args_0_
  26.7 0.0 collective-permute-done.2.args_4_.args_5_
  26.7 4.2 %shard_map.34 = (s32[4,512,128]{2,1,0:T(8,128)S(1)}, s16[4,512,128]{2,1,0:T(8,128)(2,1)S(1)}, s16[4,512,128]{2,1,0:T(8,128)(2,1)S(1)}) custom-call(s32[2]{0:T(128)S(1)} %pad_add_fusion.where, s32[2,392,512]{2,1,0:T(8,128)S(1)} %shard_map.31.args_0_, s32[2,392,512]{2,1,0:T(8,128)S(1)} %get-tuple-element.16.rest_0_.args_0_.args_1_.args_2_, ...), custom_call_target="tpu_custom_call" | custom-call | tf_op jit(solution)/shard_map/pallas_call | solution.py:339
  30.9 0.1 collective-permute-done.1.src
  31.0 0.1 shard_map.35.args_1_
  31.1 1.8 %shard_map.36 = (s32[4,512,128]{2,1,0:T(8,128)S(1)}, s16[4,512,128]{2,1,0:T(8,128)(2,1)S(1)}, s16[4,512,128]{2,1,0:T(8,128)(2,1)S(1)}) custom-call(s32[2]{0:T(128)S(1)} %pad_add_fusion.where, s32[2,392,512]{2,1,0:T(8,128)S(1)} %shard_map.31.args_0_, ...), custom_call_target="tpu_custom_call", output_to_operand_aliasing={{0}: (8, {}), {1}: (9, {}), {2}: (10, {})} | custom-call | tf_op jit(solution)/shard_map/pallas_call | solution.py:339
  32.9 3.1 %collective-permute-start.3 = (s16[4,512,128]{2,1,0:T(8,128)(2,1)S(1)}, s16[4,512,128]{2,1,0:T(8,128)(2,1)S(1)}, u32[]{:S(2)}, u32[]{:S(2)}) collective-permute-start(s16[4,512,128]{2,1,0:T(8,128)(2,1)S(1)} %get-tuple-element.24), channel_id=1, source_target_pairs={{1,2},{2,1},{3,4},{4,3},{5,6},{6,5},{7,8},{8,7},{9,10},{10,9},{11,... | collective-permute-start | bytes 1572872 | tf_op jit(solution)/shard_map/ppermute | solution.py:509
  36.0 0.1 collective-permute-start.4
  36.1 7.3 %collective-permute-done.3.args_8_ = s16[4,512,128]{2,1,0:T(8,128)(2,1)S(1)} collective-permute-done((s16[4,512,128]{2,1,0:T(8,128)(2,1)S(1)}, s16[4,512,128]{2,1,0:T(8,128)(2,1)S(1)}, u32[]{:S(2)}, u32[]{:S(2)}) %collective-permute-start.3) | collective-permute-done | bytes 524320 | tf_op jit(solution)/shard_map/ppermute | solution.py:509
  43.4 0.0 collective-permute-done.4.args_9_
  43.4 10.1 %shard_map.37 = (s32[4,512,512]{2,1,0:T(8,128)}, s32[128,128]{1,0:T(8,128)S(1)}) custom-call(s32[2]{0:T(128)S(1)} %pad_add_fusion.where, s32[2,392,512]{2,1,0:T(8,128)S(1)} %shard_map.31.args_0_, s32[2,120,512]{2,1,0:T(8,128)S(1)} %shard_map.35.args_1_, s32[2,392,512]{2,1,0:T(8,128)S(1)} %get-tuple-element.16.rest_0_.args_0_.args_1_.args_2_, ...), custom_call_target="tpu_custom_call" | custom-call | tf_op jit(solution)/shard_map/pallas_call | solution.py:474
  53.5 27.7 %all_to_all.9 = s32[128,1,128]{2,1,0:T(1,128)S(1)} all-to-all(s32[128,1,128]{2,1,0:T(1,128)S(1)} %bitcast.6), channel_id=1, replica_groups=mesh['gz_0'=4,'gz_1'=4,'gz_2'=4,'gz_3'=2] {'gz_0','gz_1','gz_2','gz_3'}, dimensions={0} | all-to-all | bytes 131072 | tf_op jit(solution)/shard_map/all_to_all | solution.py:538
  81.2 0.7 reduce_sum.9
Async XLA Ops:
  5.3 21.4 %collective-permute-start.2 = (s32[2,512,512]{2,1,0:T(8,128)S(1)}, s32[2,512,512]{2,1,0:T(8,128)S(1)}, u32[]{:S(2)}, u32[]{:S(2)}) collective-permute-start(s32[2,512,512]{2,1,0:T(8,128)S(1)} %get-tuple-element.19.args_2_.args_3_.args_4_), channel_id=1, source_target_pairs={{0,1},{1,0},{2,3},{3,2},{4,5},{5,4},{6,7},{7,6},{8,9},{9,8},{10,11... | collective-permute-start | bytes 6291464 | tf_op jit(solution)/shard_map/ppermute | solution.py:510
  6.8 19.6 %collective-permute-start = (s32[2,336,512]{2,1,0:T(8,128)S(1)}, s32[2,336,512]{2,1,0:T(8,128)S(1)}, u32[]{:S(2)}, u32[]{:S(2)}) collective-permute-start(s32[2,336,512]{2,1,0:T(8,128)S(1)} %get-tuple-element.15), channel_id=1, source_target_pairs={{1,2},{2,1},{3,4},{4,3},{5,6},{6,5},{7,8},{8,7},{9,10},{10,9},{11,... | collective-permute-start | bytes 4128776 | tf_op jit(solution)/shard_map/ppermute | solution.py:509
  9.9 21.0 %collective-permute-start.1 = (s32[2,104,512]{2,1,0:T(8,128)S(1)}, s32[2,104,512]{2,1,0:T(8,128)S(1)}, u32[]{:S(2)}, u32[]{:S(2)}) collective-permute-start(s32[2,104,512]{2,1,0:T(8,128)S(1)} %get-tuple-element.17), channel_id=1, source_target_pairs={{1,2},{2,1},{3,4},{4,3},{5,6},{6,5},{7,8},{8,7},{9,10},{10,9},{11,... | collective-permute-start | bytes 1277960 | tf_op jit(solution)/shard_map/ppermute | solution.py:509
  32.9 10.5 %collective-permute-start.3 = (s16[4,512,128]{2,1,0:T(8,128)(2,1)S(1)}, s16[4,512,128]{2,1,0:T(8,128)(2,1)S(1)}, u32[]{:S(2)}, u32[]{:S(2)}) collective-permute-start(s16[4,512,128]{2,1,0:T(8,128)(2,1)S(1)} %get-tuple-element.24), channel_id=1, source_target_pairs={{1,2},{2,1},{3,4},{4,3},{5,6},{6,5},{7,8},{8,7},{9,10},{10,9},{11,... | collective-permute-start | bytes 1572872 | tf_op jit(solution)/shard_map/ppermute | solution.py:509
  36.0 7.4 %collective-permute-start.4 = (s16[4,512,128]{2,1,0:T(8,128)(2,1)S(1)}, s16[4,512,128]{2,1,0:T(8,128)(2,1)S(1)}, u32[]{:S(2)}, u32[]{:S(2)}) collective-permute-start(s16[4,512,128]{2,1,0:T(8,128)(2,1)S(1)} %get-tuple-element.25), channel_id=1, source_target_pairs={{0,1},{1,0},{2,3},{3,2},{4,5},{5,4},{6,7},{7,6},{8,9},{9,8},{10,11... | collective-permute-start | bytes 1572872 | tf_op jit(solution)/shard_map/ppermute | solution.py:510
